TPU v7x, 32 devices: a whole 2x2x4 slice. The times are simulated.
32 devices in a mesh: groups: 2 (over x), blk: 8 (over z, y), rows: 2 (over core).
Axes of the slice: x: 2, y: 2, z: 4, core: 2. Of those that a mesh axis runs over, the one named last changes fastest.
Arguments:
- features: bfloat16 [8, 16, 256, 512], P('groups', 'rows', 'blk'), parts along dimension 0, may hold values from -60 to 60
- gain_in: float32 [512], replicated, may hold values from 0.25 to 1.75
- shift_in: float32 [512], replicated, may hold values from -3 to 3
- conv_first: bfloat16 [3, 3, 512, 256], replicated, may hold values from -0.09375 to 0.09375
- bias_first: float32 [256], replicated, may hold values from -3 to 3
- short_weight: bfloat16 [512, 256], replicated, may hold values from -0.25 to 0.25
- short_bias: float32 [256], replicated, may hold values from -3 to 3
- gains_rest: float32 [5, 256], replicated, may hold values from 0.25 to 1.75
- shifts_rest: float32 [5, 256], replicated, may hold values from -3 to 3
- convs_rest: bfloat16 [5, 3, 3, 256, 256], replicated, may hold values from -0.125 to 0.125
- biases_rest: float32 [5, 256], replicated, may hold values from -3 to 3
Outputs:
- decoded: bfloat16 [8, 16, 256, 256], P('groups', 'rows', 'blk'), parts along dimension 0
There are 2 independent parts, one for each index of `groups`. A program takes and returns all parts, laid end to end along the dimension named above; an argument that names none is the same for every part. Nothing has to cross between parts.
All inputs are finite; a program needn't handle non-finite values.
Results may differ from a plain program's by a relative error of at most 0.0065.
Values may be sent and summed in bfloat16 or wider, within the bound.
A program may use at most 128 MiB of HBM per device.

v0:
```python
import jax
import jax.numpy as jnp
from jax import lax
from jax.sharding import PartitionSpec as P

GROUPS = 32
RESNETS = 3
EPS = 1e-06


def with_halo(block, sides, width, periodic):
    for axis, dim in sides:
        count = lax.axis_size(axis)
        forward = [(i, i + 1) for i in range(count - 1)]
        if periodic:
            forward.append((count - 1, 0))
        backward = [(target, source) for source, target in forward]
        low = lax.ppermute(
            lax.slice_in_dim(block, block.shape[dim] - width, None, axis=dim), axis, forward
        )
        high = lax.ppermute(lax.slice_in_dim(block, 0, width, axis=dim), axis, backward)
        block = jnp.concatenate([low, block, high], axis=dim)
    return block


def group_totals(values, groups):
    shaped = values.reshape(values.shape[0], -1, groups, values.shape[3] // groups)
    return jnp.sum(shaped, axis=(1, 3))


def per_channel(stat, channels):
    return jnp.repeat(stat, channels // stat.shape[1], axis=1)[:, None, None, :]


def norm_act(values, inner, gain, shift):
    channels = values.shape[3]
    count = (
        inner.shape[1]
        * inner.shape[2]
        * lax.axis_size("blk")
        * lax.axis_size("rows")
        * (channels // GROUPS)
    )
    total, square = lax.psum(
        (group_totals(inner, GROUPS), group_totals(inner * inner, GROUPS)), ("blk", "rows")
    )
    center = total / count
    spread = square / count - center * center
    scaled = (values - per_channel(center, channels)) * per_channel(
        lax.rsqrt(spread + EPS), channels
    ) * gain + shift
    return scaled * jax.nn.sigmoid(scaled)


def convolve(padded, weight, bias):
    height = padded.shape[1] - 2
    width = padded.shape[2] - 2
    inputs = weight.shape[2]
    total = jnp.zeros((padded.shape[0] * height * width, weight.shape[3]), jnp.float32)
    for shift_row in range(3):
        band = padded[:, shift_row : shift_row + height]
        stacked = jnp.concatenate(
            [band[:, :, shift_col : shift_col + width] for shift_col in range(3)], axis=3
        )
        total = total + jnp.dot(
            stacked.reshape(-1, 3 * inputs),
            weight[shift_row].reshape(3 * inputs, weight.shape[3]),
            preferred_element_type=jnp.float32,
        )
    return total.reshape(padded.shape[0], height, width, weight.shape[3]) + bias


def extend_once(field):
    tall = with_halo(field, (("rows", 1),), 1, False)
    return with_halo(tall, (("blk", 2),), 1, True)


def body(
    features,
    gain_in,
    shift_in,
    conv_first,
    bias_first,
    short_weight,
    short_bias,
    gains_rest,
    shifts_rest,
    convs_rest,
    biases_rest,
):
    stream = features
    for block in range(RESNETS):
        if block == 0:
            first = (gain_in, shift_in, conv_first, bias_first)
        else:
            first = (
                gains_rest[2 * block - 1],
                shifts_rest[2 * block - 1],
                convs_rest[2 * block - 1],
                biases_rest[2 * block - 1],
            )
        second = (
            gains_rest[2 * block],
            shifts_rest[2 * block],
            convs_rest[2 * block],
            biases_rest[2 * block],
        )
        source = stream.astype(jnp.float32)
        active = norm_act(source, source, first[0], first[1]).astype(jnp.bfloat16)
        inner = convolve(extend_once(active), first[2], first[3]).astype(jnp.bfloat16)
        middle = inner.astype(jnp.float32)
        active_two = norm_act(middle, middle, second[0], second[1]).astype(jnp.bfloat16)
        branch = convolve(extend_once(active_two), second[2], second[3])
        if block == 0:
            flat = stream.reshape(-1, stream.shape[3])
            skip = jnp.dot(flat, short_weight, preferred_element_type=jnp.float32) + short_bias
            skip = skip.reshape(
                stream.shape[0], stream.shape[1], stream.shape[2], short_weight.shape[1]
            )
        else:
            skip = stream.astype(jnp.float32)
        stream = (skip + branch).astype(jnp.bfloat16)
    return stream


def solution(mesh):
    placed = (P("groups", "rows", "blk", None), P(), P(), P(), P(), P(), P(), P(), P(), P(), P())
    return jax.shard_map(
        body,
        mesh=mesh,
        in_specs=placed,
        out_specs=P("groups", "rows", "blk", None),
        check_vma=False,
    )
```

profile of v0, /device:TPU:0, one launch (start us, length us, event | category | flops | bytes accessed | tf_op | source)
XLA Modules:
  0.0 329.6 jit_solution(16887478936183795066)
XLA Ops:
  0.0 1.6 convert_reduce_fusion
  2.0 35.0 %all-reduce.5 = (f32[4,32]{1,0:T(4,128)S(1)}, f32[4,32]{1,0:T(4,128)S(1)}) all-reduce(f32[4,32]{1,0:T(4,128)S(1)} %reduce_sum.127, f32[4,32]{1,0:T(4,128)S(1)} %reduce_sum.124), channel_id=1, replica_groups=mesh['groups'=2,'blk'=8,'rows'=2] {'blk','rows'}, use_global_device_ids=true, to_apply=%region_5.0 | all-reduce | flops 256 | bytes 2048 | tf_op jit(solution)/shard_map/psum | solution.py:44
  37.4 0.7 fusion.12
  38.2 1.6 collective-permute-start
  39.7 1.3 collective-permute-start.1
  41.0 2.9 fusion.68
  44.0 2.6 fusion.67
  46.6 0.8 pad_maximum_fusion.26
  47.4 4.7 %collective-permute-start.3 = (bf16[4,10,1,512]{3,2,1,0:T(2,128)(2,1)S(1)}, bf16[4,10,1,512]{3,2,1,0:T(2,128)(2,1)}, u32[]{:S(2)}, u32[]{:S(2)}) collective-permute-start(bf16[4,10,1,512]{3,2,1,0:T(2,128)(2,1)S(1)} %get-tuple-element.65), channel_id=1, source_target_pairs={{2,0},{4,2},{6,4},{8,6},{10,8},{12,10},{14,12},{0,14},{3,1},{5,3},... | collective-permute-start | bytes 122888 | tf_op jit(solution)/shard_map/ppermute | solution.py:21
  52.2 3.3 %collective-permute-done.2 = bf16[4,10,1,512]{3,2,1,0:T(2,128)(2,1)} collective-permute-done((bf16[4,10,1,512]{3,2,1,0:T(2,128)(2,1)}, bf16[4,10,1,512]{3,2,1,0:T(2,128)(2,1)}, u32[]{:S(2)}, u32[]{:S(2)}) %collective-permute-start.2) | collective-permute-done | bytes 40992 | tf_op jit(solution)/shard_map/ppermute | solution.py:18
  55.5 1.7 maximum_maximum_fusion
  57.2 1.0 fusion.69
  58.2 1.0 fusion.3
  59.4 1.0 fusion.89
  60.5 1.0 fusion.90
  61.5 1.0 fusion.39
  62.5 1.3 copy.36
  63.8 1.7 reshape.209
  65.5 0.7 convert_reduce_fusion.5
  66.4 33.6 %all-reduce.4 = (f32[4,32]{1,0:T(4,128)S(1)}, f32[4,32]{1,0:T(4,128)S(1)}) all-reduce(f32[4,32]{1,0:T(4,128)S(1)} %copy.38, f32[4,32]{1,0:T(4,128)S(1)} %copy.37), channel_id=1, replica_groups=mesh['groups'=2,'blk'=8,'rows'=2] {'blk','rows'}, use_global_device_ids=true, to_apply=%region_9.0 | all-reduce | flops 256 | bytes 2048 | tf_op jit(solution)/shard_map/psum | solution.py:44
  100.8 1.3 collective-permute-start.4
  102.1 1.3 collective-permute-start.5
  103.9 1.4 collective-permute-done.5
  105.4 4.7 %collective-permute-start.7 = (bf16[4,10,1,256]{3,2,1,0:T(2,128)(2,1)S(1)}, bf16[4,10,1,256]{3,2,1,0:T(2,128)(2,1)S(1)}, u32[]{:S(2)}, u32[]{:S(2)}) collective-permute-start(bf16[4,10,1,256]{3,2,1,0:T(2,128)(2,1)S(1)} %get-tuple-element.120), channel_id=1, source_target_pairs={{2,0},{4,2},{6,4},{8,6},{10,8},{12,10},{14,12},{0,14},{3,1},{5,3},... | collective-permute-start | bytes 61448 | tf_op jit(solution)/shard_map/ppermute | solution.py:21
  110.5 1.5 reshape.214
  116.7 1.4 reshape.215
  118.1 3.0 convert_reduce_fusion.1
  121.3 32.5 %all-reduce.3 = (f32[4,32]{1,0:T(4,128)S(1)}, f32[4,32]{1,0:T(4,128)S(1)}) all-reduce(f32[4,32]{1,0:T(4,128)S(1)} %copy.42, f32[4,32]{1,0:T(4,128)S(1)} %copy.41), channel_id=1, replica_groups=mesh['groups'=2,'blk'=8,'rows'=2] {'blk','rows'}, use_global_device_ids=true, to_apply=%region_13.0 | all-reduce | flops 256 | bytes 2048 | tf_op jit(solution)/shard_map/psum | solution.py:44
  154.2 1.2 fusion.49
  155.4 1.3 collective-permute-start.8
  156.7 1.3 collective-permute-start.9
  158.1 1.8 collective-permute-done.9
  160.0 4.7 %collective-permute-start.11 = (bf16[4,10,1,256]{3,2,1,0:T(2,128)(2,1)S(1)}, bf16[4,10,1,256]{3,2,1,0:T(2,128)(2,1)S(1)}, u32[]{:S(2)}, u32[]{:S(2)}) collective-permute-start(bf16[4,10,1,256]{3,2,1,0:T(2,128)(2,1)S(1)} %get-tuple-element.116), channel_id=1, source_target_pairs={{2,0},{4,2},{6,4},{8,6},{10,8},{12,10},{14,12},{0,14},{3,1},{5,3},... | collective-permute-start | bytes 61448 | tf_op jit(solution)/shard_map/ppermute | solution.py:21
  164.8 1.9 collective-permute-done.10
  170.4 0.6 fusion.37
  171.0 1.3 copy.43
  172.3 1.7 reshape.220
  174.0 0.7 convert_reduce_fusion.4
  174.9 32.5 %all-reduce.2 = (f32[4,32]{1,0:T(4,128)S(1)}, f32[4,32]{1,0:T(4,128)S(1)}) all-reduce(f32[4,32]{1,0:T(4,128)S(1)} %copy.45, f32[4,32]{1,0:T(4,128)S(1)} %copy.44), channel_id=1, replica_groups=mesh['groups'=2,'blk'=8,'rows'=2] {'blk','rows'}, use_global_device_ids=true, to_apply=%region_17.0 | all-reduce | flops 256 | bytes 2048 | tf_op jit(solution)/shard_map/psum | solution.py:44
  208.2 1.3 collective-permute-start.12
  209.5 1.3 collective-permute-start.13
  210.8 1.8 collective-permute-done.13
  212.8 4.7 %collective-permute-start.15 = (bf16[4,10,1,256]{3,2,1,0:T(2,128)(2,1)S(1)}, bf16[4,10,1,256]{3,2,1,0:T(2,128)(2,1)S(1)}, u32[]{:S(2)}, u32[]{:S(2)}) collective-permute-start(bf16[4,10,1,256]{3,2,1,0:T(2,128)(2,1)S(1)} %get-tuple-element.112), channel_id=1, source_target_pairs={{2,0},{4,2},{6,4},{8,6},{10,8},{12,10},{14,12},{0,14},{3,1},{5,3},... | collective-permute-start | bytes 61448 | tf_op jit(solution)/shard_map/ppermute | solution.py:21
  217.6 1.9 collective-permute-done.14
  223.2 0.6 fusion.36
  223.8 1.3 copy.46
  225.1 1.8 reshape.225
  226.9 0.8 convert_reduce_fusion.3
  227.9 32.5 %all-reduce.1 = (f32[4,32]{1,0:T(4,128)S(1)}, f32[4,32]{1,0:T(4,128)S(1)}) all-reduce(f32[4,32]{1,0:T(4,128)S(1)} %copy.48, f32[4,32]{1,0:T(4,128)S(1)} %copy.47), channel_id=1, replica_groups=mesh['groups'=2,'blk'=8,'rows'=2] {'blk','rows'}, use_global_device_ids=true, to_apply=%region_21.0 | all-reduce | flops 256 | bytes 2048 | tf_op jit(solution)/shard_map/psum | solution.py:44
  260.8 1.2 fusion.60
  262.0 1.3 collective-permute-start.16
  263.3 1.3 collective-permute-start.17
  264.6 1.8 collective-permute-done.17
  266.6 4.7 %collective-permute-start.19 = (bf16[4,10,1,256]{3,2,1,0:T(2,128)(2,1)S(1)}, bf16[4,10,1,256]{3,2,1,0:T(2,128)(2,1)S(1)}, u32[]{:S(2)}, u32[]{:S(2)}) collective-permute-start(bf16[4,10,1,256]{3,2,1,0:T(2,128)(2,1)S(1)} %get-tuple-element.108), channel_id=1, source_target_pairs={{2,0},{4,2},{6,4},{8,6},{10,8},{12,10},{14,12},{0,14},{3,1},{5,3},... | collective-permute-start | bytes 61448 | tf_op jit(solution)/shard_map/ppermute | solution.py:21
  271.4 1.9 collective-permute-done.18
  278.4 0.7 convert_reduce_fusion.2
  279.3 32.5 %all-reduce = (f32[4,32]{1,0:T(4,128)S(1)}, f32[4,32]{1,0:T(4,128)S(1)}) all-reduce(f32[4,32]{1,0:T(4,128)S(1)} %copy.51, f32[4,32]{1,0:T(4,128)S(1)} %copy.50), channel_id=1, replica_groups=mesh['groups'=2,'blk'=8,'rows'=2] {'blk','rows'}, use_global_device_ids=true, to_apply=%region_25.26 | all-reduce | flops 256 | bytes 2048 | tf_op jit(solution)/shard_map/psum | solution.py:44
  312.6 1.3 collective-permute-start.20
  313.9 1.3 collective-permute-start.21
  315.2 1.8 collective-permute-done.21
  317.2 4.7 %collective-permute-start.23 = (bf16[4,10,1,256]{3,2,1,0:T(2,128)(2,1)S(1)}, bf16[4,10,1,256]{3,2,1,0:T(2,128)(2,1)S(1)}, u32[]{:S(2)}, u32[]{:S(2)}) collective-permute-start(bf16[4,10,1,256]{3,2,1,0:T(2,128)(2,1)S(1)} %get-tuple-element.104), channel_id=1, source_target_pairs={{2,0},{4,2},{6,4},{8,6},{10,8},{12,10},{14,12},{0,14},{3,1},{5,3},... | collective-permute-start | bytes 61448 | tf_op jit(solution)/shard_map/ppermute | solution.py:21
  321.9 2.0 collective-permute-done.22
  327.6 0.6 fusion.34
  328.6 1.0 fusion.61
  (185 shorter events, 27.7 us)
Async XLA Ops:
  0.0 103.4 %copy-start = (bf16[512,256]{1,0:T(8,128)(2,1)S(1)}, bf16[512,256]{1,0:T(8,128)(2,1)}, u32[]{:S(2)}) copy-start(bf16[512,256]{1,0:T(8,128)(2,1)} %param.16) | copy-start | bytes 786436
  0.0 37.4 %copy-start.2 = (bf16[4,8,32,512]{3,2,1,0:T(8,128)(2,1)S(1)}, bf16[4,8,32,512]{3,2,1,0:T(8,128)(2,1)}, u32[]{:S(2)}) copy-start(bf16[4,8,32,512]{3,2,1,0:T(8,128)(2,1)} %param.11) | copy-start | bytes 3145732
  0.0 37.4 %copy-start.29 = (f32[512]{0:T(512)S(1)}, f32[512]{0:T(512)}, u32[]{:S(2)}) copy-start(f32[512]{0:T(512)} %param.12) | copy-start | bytes 6148
  0.0 37.4 %copy-start.28 = (f32[512]{0:T(512)S(1)}, f32[512]{0:T(512)}, u32[]{:S(2)}) copy-start(f32[512]{0:T(512)} %param.13) | copy-start | bytes 6148
  37.4 6.6 %copy-start.3 = (bf16[5,3,3,256,256]{4,3,2,1,0:T(8,128)(2,1)S(1)}, bf16[5,3,3,256,256]{4,3,2,1,0:T(8,128)(2,1)}, u32[]{:S(2)}) copy-start(bf16[5,3,3,256,256]{4,3,2,1,0:T(8,128)(2,1)} %param.20) | copy-start | bytes 17694724
  38.2 8.4 %collective-permute-start = (bf16[4,1,32,512]{3,2,1,0:T(8,128)(2,1)S(1)}, bf16[4,1,32,512]{3,2,1,0:T(8,128)(2,1)S(1)}, u32[]{:S(2)}, u32[]{:S(2)}) collective-permute-start(bf16[4,1,32,512]{3,2,1,0:T(8,128)(2,1)S(1)} %get-tuple-element.69), channel_id=1, source_target_pairs={{0,1},{2,3},{4,5},{6,7},{8,9},{10,11},{12,13},{14,15},{16,17},{18,... | collective-permute-start | bytes 393224 | tf_op jit(solution)/shard_map/ppermute | solution.py:18
  39.7 6.9 %collective-permute-start.1 = (bf16[4,1,32,512]{3,2,1,0:T(8,128)(2,1)S(1)}, bf16[4,1,32,512]{3,2,1,0:T(8,128)(2,1)S(1)}, u32[]{:S(2)}, u32[]{:S(2)}) collective-permute-start(bf16[4,1,32,512]{3,2,1,0:T(8,128)(2,1)S(1)} %get-tuple-element.70), channel_id=1, source_target_pairs={{1,0},{3,2},{5,4},{7,6},{9,8},{11,10},{13,12},{15,14},{17,16},{19,... | collective-permute-start | bytes 393224 | tf_op jit(solution)/shard_map/ppermute | solution.py:21
  44.0 2.6 copy-start.26
  44.0 8.1 %copy-start.27 = (f32[5,256]{1,0:T(8,128)S(1)}, f32[5,256]{1,0:T(8,128)}, u32[]{:S(2)}) copy-start(f32[5,256]{1,0:T(8,128)} %param.18) | copy-start | bytes 15364
  44.0 8.1 %copy-start.24 = (f32[256]{0:T(256)S(1)}, f32[256]{0:T(256)}, u32[]{:S(2)}) copy-start(f32[256]{0:T(256)} %param.15) | copy-start | bytes 3076
  47.4 8.2 %collective-permute-start.2 = (bf16[4,10,1,512]{3,2,1,0:T(2,128)(2,1)}, bf16[4,10,1,512]{3,2,1,0:T(2,128)(2,1)}, u32[]{:S(2)}, u32[]{:S(2)}) collective-permute-start(bf16[4,10,1,512]{3,2,1,0:T(2,128)(2,1)} %get-tuple-element.64), channel_id=1, source_target_pairs={{0,2},{2,4},{4,6},{6,8},{8,10},{10,12},{12,14},{14,0},{1,3},{3,5},... | collective-permute-start | bytes 122888 | tf_op jit(solution)/shard_map/ppermute | solution.py:18
  47.4 8.2 %collective-permute-start.3 = (bf16[4,10,1,512]{3,2,1,0:T(2,128)(2,1)S(1)}, bf16[4,10,1,512]{3,2,1,0:T(2,128)(2,1)}, u32[]{:S(2)}, u32[]{:S(2)}) collective-permute-start(bf16[4,10,1,512]{3,2,1,0:T(2,128)(2,1)S(1)} %get-tuple-element.65), channel_id=1, source_target_pairs={{2,0},{4,2},{6,4},{8,6},{10,8},{12,10},{14,12},{0,14},{3,1},{5,3},... | collective-permute-start | bytes 122888 | tf_op jit(solution)/shard_map/ppermute | solution.py:21
  58.2 1.1 copy-start.23
  59.4 1.1 copy-start.22
  65.5 37.9 %copy-start.30 = (f32[256]{0:T(256)S(1)}, f32[256]{0:T(256)}, u32[]{:S(2)}) copy-start(f32[256]{0:T(256)} %param.17) | copy-start | bytes 3076
  100.8 9.3 %copy-start.25 = (f32[5,256]{1,0:T(8,128)S(1)}, f32[5,256]{1,0:T(8,128)}, u32[]{:S(2)}) copy-start(f32[5,256]{1,0:T(8,128)} %param.21) | copy-start | bytes 15364
  100.8 3.1 collective-permute-start.4
  102.1 3.1 collective-permute-start.5
  105.3 6.8 %collective-permute-start.6 = (bf16[4,10,1,256]{3,2,1,0:T(2,128)(2,1)S(1)}, bf16[4,10,1,256]{3,2,1,0:T(2,128)(2,1)S(1)}, u32[]{:S(2)}, u32[]{:S(2)}) collective-permute-start(bf16[4,10,1,256]{3,2,1,0:T(2,128)(2,1)S(1)} %get-tuple-element.119), channel_id=1, source_target_pairs={{0,2},{2,4},{4,6},{6,8},{8,10},{10,12},{12,14},{14,0},{1,3},{3,5},... | collective-permute-start | bytes 61448 | tf_op jit(solution)/shard_map/ppermute | solution.py:18
  105.4 6.7 %collective-permute-start.7 = (bf16[4,10,1,256]{3,2,1,0:T(2,128)(2,1)S(1)}, bf16[4,10,1,256]{3,2,1,0:T(2,128)(2,1)S(1)}, u32[]{:S(2)}, u32[]{:S(2)}) collective-permute-start(bf16[4,10,1,256]{3,2,1,0:T(2,128)(2,1)S(1)} %get-tuple-element.120), channel_id=1, source_target_pairs={{2,0},{4,2},{6,4},{8,6},{10,8},{12,10},{14,12},{0,14},{3,1},{5,3},... | collective-permute-start | bytes 61448 | tf_op jit(solution)/shard_map/ppermute | solution.py:21
  113.2 1.0 copy-start.21
  113.6 1.1 copy-start.20
  114.7 1.0 copy-start.11
  155.4 2.6 collective-permute-start.8
  156.7 3.1 collective-permute-start.9
  160.0 6.8 %collective-permute-start.10 = (bf16[4,10,1,256]{3,2,1,0:T(2,128)(2,1)S(1)}, bf16[4,10,1,256]{3,2,1,0:T(2,128)(2,1)S(1)}, u32[]{:S(2)}, u32[]{:S(2)}) collective-permute-start(bf16[4,10,1,256]{3,2,1,0:T(2,128)(2,1)S(1)} %get-tuple-element.115), channel_id=1, source_target_pairs={{0,2},{2,4},{4,6},{6,8},{8,10},{10,12},{12,14},{14,0},{1,3},{3,5},... | collective-permute-start | bytes 61448 | tf_op jit(solution)/shard_map/ppermute | solution.py:18
  160.0 6.7 %collective-permute-start.11 = (bf16[4,10,1,256]{3,2,1,0:T(2,128)(2,1)S(1)}, bf16[4,10,1,256]{3,2,1,0:T(2,128)(2,1)S(1)}, u32[]{:S(2)}, u32[]{:S(2)}) collective-permute-start(bf16[4,10,1,256]{3,2,1,0:T(2,128)(2,1)S(1)} %get-tuple-element.116), channel_id=1, source_target_pairs={{2,0},{4,2},{6,4},{8,6},{10,8},{12,10},{14,12},{0,14},{3,1},{5,3},... | collective-permute-start | bytes 61448 | tf_op jit(solution)/shard_map/ppermute | solution.py:21
  167.8 1.0 copy-start.19
  168.3 1.1 copy-start.18
  169.4 1.0 copy-start.10
  208.2 2.6 collective-permute-start.12
  209.5 3.1 collective-permute-start.13
  212.7 6.8 %collective-permute-start.14 = (bf16[4,10,1,256]{3,2,1,0:T(2,128)(2,1)S(1)}, bf16[4,10,1,256]{3,2,1,0:T(2,128)(2,1)S(1)}, u32[]{:S(2)}, u32[]{:S(2)}) collective-permute-start(bf16[4,10,1,256]{3,2,1,0:T(2,128)(2,1)S(1)} %get-tuple-element.111), channel_id=1, source_target_pairs={{0,2},{2,4},{4,6},{6,8},{8,10},{10,12},{12,14},{14,0},{1,3},{3,5},... | collective-permute-start | bytes 61448 | tf_op jit(solution)/shard_map/ppermute | solution.py:18
  212.8 6.7 %collective-permute-start.15 = (bf16[4,10,1,256]{3,2,1,0:T(2,128)(2,1)S(1)}, bf16[4,10,1,256]{3,2,1,0:T(2,128)(2,1)S(1)}, u32[]{:S(2)}, u32[]{:S(2)}) collective-permute-start(bf16[4,10,1,256]{3,2,1,0:T(2,128)(2,1)S(1)} %get-tuple-element.112), channel_id=1, source_target_pairs={{2,0},{4,2},{6,4},{8,6},{10,8},{12,10},{14,12},{0,14},{3,1},{5,3},... | collective-permute-start | bytes 61448 | tf_op jit(solution)/shard_map/ppermute | solution.py:21
  220.6 1.0 copy-start.17
  221.1 1.1 copy-start.16
  222.2 1.0 copy-start.9
  223.8 3.1 copy-start.5
  225.1 35.6 %copy-start.4 = (bf16[4,8,32,256]{3,2,1,0:T(8,128)(2,1)S(1)}, bf16[4,8,32,256]{3,2,1,0:T(8,128)(2,1)}, u32[]{:S(2)}) copy-start(bf16[4,8,32,256]{3,2,1,0:T(8,128)(2,1)} %get-tuple-element.36) | copy-start | bytes 1572868
  262.0 2.6 collective-permute-start.16
  263.3 3.1 collective-permute-start.17
  266.5 6.8 %collective-permute-start.18 = (bf16[4,10,1,256]{3,2,1,0:T(2,128)(2,1)S(1)}, bf16[4,10,1,256]{3,2,1,0:T(2,128)(2,1)S(1)}, u32[]{:S(2)}, u32[]{:S(2)}) collective-permute-start(bf16[4,10,1,256]{3,2,1,0:T(2,128)(2,1)S(1)} %get-tuple-element.107), channel_id=1, source_target_pairs={{0,2},{2,4},{4,6},{6,8},{8,10},{10,12},{12,14},{14,0},{1,3},{3,5},... | collective-permute-start | bytes 61448 | tf_op jit(solution)/shard_map/ppermute | solution.py:18
  266.6 6.7 %collective-permute-start.19 = (bf16[4,10,1,256]{3,2,1,0:T(2,128)(2,1)S(1)}, bf16[4,10,1,256]{3,2,1,0:T(2,128)(2,1)S(1)}, u32[]{:S(2)}, u32[]{:S(2)}) collective-permute-start(bf16[4,10,1,256]{3,2,1,0:T(2,128)(2,1)S(1)} %get-tuple-element.108), channel_id=1, source_target_pairs={{2,0},{4,2},{6,4},{8,6},{10,8},{12,10},{14,12},{0,14},{3,1},{5,3},... | collective-permute-start | bytes 61448 | tf_op jit(solution)/shard_map/ppermute | solution.py:21
  274.4 1.0 copy-start.15
  274.9 1.1 copy-start.14
  276.0 1.0 copy-start.8
  312.6 2.6 collective-permute-start.20
  313.9 3.1 collective-permute-start.21
  317.1 6.8 %collective-permute-start.22 = (bf16[4,10,1,256]{3,2,1,0:T(2,128)(2,1)S(1)}, bf16[4,10,1,256]{3,2,1,0:T(2,128)(2,1)S(1)}, u32[]{:S(2)}, u32[]{:S(2)}) collective-permute-start(bf16[4,10,1,256]{3,2,1,0:T(2,128)(2,1)S(1)} %get-tuple-element.103), channel_id=1, source_target_pairs={{0,2},{2,4},{4,6},{6,8},{8,10},{10,12},{12,14},{14,0},{1,3},{3,5},... | collective-permute-start | bytes 61448 | tf_op jit(solution)/shard_map/ppermute | solution.py:18
  317.2 6.7 %collective-permute-start.23 = (bf16[4,10,1,256]{3,2,1,0:T(2,128)(2,1)S(1)}, bf16[4,10,1,256]{3,2,1,0:T(2,128)(2,1)S(1)}, u32[]{:S(2)}, u32[]{:S(2)}) collective-permute-start(bf16[4,10,1,256]{3,2,1,0:T(2,128)(2,1)S(1)} %get-tuple-element.104), channel_id=1, source_target_pairs={{2,0},{4,2},{6,4},{8,6},{10,8},{12,10},{14,12},{0,14},{3,1},{5,3},... | collective-permute-start | bytes 61448 | tf_op jit(solution)/shard_map/ppermute | solution.py:21
  325.0 1.0 copy-start.13
  325.5 1.1 copy-start.12
  326.6 1.0 copy-start.7
  327.6 1.0 copy-start.6
  327.6 2.0 copy-start.1
where the time goes:
time: 331 us; the launch traced here: 330 us
  blocking collectives  199 us (60%)
  starting transfers between devices  44.3 us (13%)
  local copies, waits for them, and re-layouts  31.8 us (10%)
  other arithmetic  21.7 us (7%)
  waiting for transfers between devices  19.8 us (6%)
  matrix products  12.2 us (4%)
    psum x6, blocking collectives, norm_act(): lax.psum((group_totals(inner, GROUPS), group_totals(inner * inner, GROUPS...  199 us
    ppermute x12, starting transfers between devices, with_halo(): lax.ppermute(lax.slice_in_dim(block, 0, width, axis=dim), axis, backward)  36 us
    dot_general x18, matrix products, convolve(): jnp.dot(stacked.reshape(-1, 3 * inputs), weight[shift_row].reshape(3 * in...  11.8 us
    ppermute x12, waiting for transfers between devices, with_halo(): lax.ppermute(lax.slice_in_dim(block, block.shape[dim] - width, None, axis...  11.1 us
    ppermute x12, waiting for transfers between devices, with_halo(): lax.ppermute(lax.slice_in_dim(block, 0, width, axis=dim), axis, backward)  8.75 us
    ppermute x12, starting transfers between devices, with_halo(): lax.ppermute(lax.slice_in_dim(block, block.shape[dim] - width, None, axis...  8.32 us
    reduce_sum x8, other arithmetic, group_totals(): return jnp.sum(shaped, axis=(1, 3))  7.68 us
    reshape x5, local copies, waits for them, and re-layouts, convolve(): return total.reshape(padded.shape[0], height, width, weight.shape[3]) + bias  7.09 us
  transfers between devices with their start and end apart: 24, of which 11 were waited for; matrix products, arithmetic and copies ran while one was open for 2% of the time, Pallas kernels for 0%

commit v1 on v0

--- a/solution.py
+++ b/solution.py
@@ -1,3 +1,4 @@
+import functools
 import jax
 import jax.numpy as jnp
 from jax import lax
@@ -6,6 +7,13 @@
 GROUPS = 32
 RESNETS = 3
 EPS = 1e-06
+
+
+def arrange_heads(v0, comm_axis, named_axis):
+    return lax.psum(lax.psum(v0, axis_name=comm_axis), axis_name=named_axis)
+
+
+_name_strings = functools.partial(arrange_heads, comm_axis="rows", named_axis="blk")
 
 
 def with_halo(block, sides, width, periodic):
@@ -41,8 +49,8 @@
         * lax.axis_size("rows")
         * (channels // GROUPS)
     )
-    total, square = lax.psum(
-        (group_totals(inner, GROUPS), group_totals(inner * inner, GROUPS)), ("blk", "rows")
+    total, square = _name_strings(
+        (group_totals(inner, GROUPS), group_totals(inner * inner, GROUPS))
     )
     center = total / count
     spread = square / count - center * center

time: 331 us -> 276 us (0.83)
  blocking collectives: 199 us -> 147 us
  local copies, waits for them, and re-layouts: 31.8 us -> 27.3 us
    psum x6 -> x12, blocking collectives: 199 us -> 147 us  [arrange_heads(): return lax.psum(lax.psum(v0, axis_name=comm_axis), axis_name=named_axis)]
  transfers between devices with their start and end apart: 24 -> 24, of which waited for: 11 -> 11; matrix products, arithmetic and copies ran while one was open for 2% -> 3% of each run, Pallas kernels for 0% -> 0%
where the time goes in v1:
time: 276 us; the launch traced here: 274 us
  blocking collectives  147 us (53%)
  starting transfers between devices  44.3 us (16%)
  local copies, waits for them, and re-layouts  27.3 us (10%)
  other arithmetic  22.8 us (8%)
  waiting for transfers between devices  19.8 us (7%)
  matrix products  12.2 us (4%)
    psum x12, blocking collectives, arrange_heads(): return lax.psum(lax.psum(v0, axis_name=comm_axis), axis_name=named_axis)  147 us
    ppermute x12, starting transfers between devices, with_halo(): lax.ppermute(lax.slice_in_dim(block, 0, width, axis=dim), axis, backward)  36 us
    dot_general x18, matrix products, convolve(): jnp.dot(stacked.reshape(-1, 3 * inputs), weight[shift_row].reshape(3 * in...  11.8 us
    ppermute x12, waiting for transfers between devices, with_halo(): lax.ppermute(lax.slice_in_dim(block, block.shape[dim] - width, None, axis...  11.1 us
    reduce_sum x8, other arithmetic, group_totals(): return jnp.sum(shaped, axis=(1, 3))  8.77 us
    ppermute x12, waiting for transfers between devices, with_halo(): lax.ppermute(lax.slice_in_dim(block, 0, width, axis=dim), axis, backward)  8.75 us
    ppermute x12, starting transfers between devices, with_halo(): lax.ppermute(lax.slice_in_dim(block, block.shape[dim] - width, None, axis...  8.32 us
    slice x2, local copies, waits for them, and re-layouts, convolve(): weight[shift_row].reshape(3 * inputs, weight.shape[3])  5.53 us
  transfers between devices with their start and end apart: 24, of which 11 were waited for; matrix products, arithmetic and copies ran while one was open for 3% of the time, Pallas kernels for 0%

profile of v1, /device:TPU:0, one launch (start us, length us, event | category | flops | bytes accessed | tf_op | source)
XLA Modules:
  0.0 274.4 jit_solution(15798554053953337799)
XLA Ops:
  0.0 1.6 convert_reduce_fusion
  2.0 2.6 all-reduce.11
  4.7 23.0 %all-reduce.5 = (f32[4,32]{1,0:T(4,128)S(1)}, f32[4,32]{1,0:T(4,128)S(1)}) all-reduce(f32[4,32]{1,0:T(4,128)S(1)} %get-tuple-element.43, f32[4,32]{1,0:T(4,128)S(1)} %get-tuple-element.44), channel_id=1, replica_groups=mesh['groups'=2,'blk'=8,'rows'=2] {'blk'}, use_global_device_ids=true, to_apply=%region_7.0 | all-reduce | flops 256 | bytes 2048 | tf_op jit(solution)/shard_map/psum | solution.py:13
  28.1 0.7 fusion.12
  28.8 1.6 collective-permute-start
  30.4 1.3 collective-permute-start.1
  31.7 3.0 %fusion.68 = (bf16[1,3,512,256]{3,2,1,0:T(8,128)(2,1)S(1)}, bf16[1,3,512,256]{3,2,1,0:T(8,128)(2,1)}, bf16[1,3,512,256]{3,2,1,0:T(8,128)(2,1)}) fusion(bf16[3,3,512,256]{3,2,1,0:T(8,128)(2,1)} %param.14), kind=kLoop, calls=%fused_computation.167 | loop fusion | bytes 4718592 | tf_op jit(solution)/shard_map/slice | solution.py:75
  34.7 2.6 fusion.67
  37.3 0.8 pad_maximum_fusion.26
  38.0 4.7 %collective-permute-start.3 = (bf16[4,10,1,512]{3,2,1,0:T(2,128)(2,1)S(1)}, bf16[4,10,1,512]{3,2,1,0:T(2,128)(2,1)}, u32[]{:S(2)}, u32[]{:S(2)}) collective-permute-start(bf16[4,10,1,512]{3,2,1,0:T(2,128)(2,1)S(1)} %get-tuple-element.77), channel_id=1, source_target_pairs={{2,0},{4,2},{6,4},{8,6},{10,8},{12,10},{14,12},{0,14},{3,1},{5,3},... | collective-permute-start | bytes 122888 | tf_op jit(solution)/shard_map/ppermute | solution.py:29
  42.8 3.3 %collective-permute-done.2 = bf16[4,10,1,512]{3,2,1,0:T(2,128)(2,1)} collective-permute-done((bf16[4,10,1,512]{3,2,1,0:T(2,128)(2,1)}, bf16[4,10,1,512]{3,2,1,0:T(2,128)(2,1)}, u32[]{:S(2)}, u32[]{:S(2)}) %collective-permute-start.2) | collective-permute-done | bytes 40992 | tf_op jit(solution)/shard_map/ppermute | solution.py:26
  46.2 1.7 maximum_maximum_fusion
  47.9 1.0 fusion.69
  48.9 1.0 fusion.3
  50.0 1.0 fusion.89
  51.2 1.0 fusion.90
  52.1 1.0 fusion.39
  53.1 1.3 copy.36
  54.5 1.7 reshape.209
  56.2 0.7 convert_reduce_fusion.5
  57.0 2.5 all-reduce.10
  59.5 21.7 %all-reduce.4 = (f32[4,32]{1,0:T(4,128)S(1)}, f32[4,32]{1,0:T(4,128)S(1)}) all-reduce(f32[4,32]{1,0:T(4,128)S(1)} %get-tuple-element.41, f32[4,32]{1,0:T(4,128)S(1)} %get-tuple-element.42), channel_id=1, replica_groups=mesh['groups'=2,'blk'=8,'rows'=2] {'blk'}, use_global_device_ids=true, to_apply=%region_13.0 | all-reduce | flops 256 | bytes 2048 | tf_op jit(solution)/shard_map/psum | solution.py:13
  81.9 1.3 collective-permute-start.4
  83.2 1.3 collective-permute-start.5
  85.0 1.4 collective-permute-done.5
  86.5 4.7 %collective-permute-start.7 = (bf16[4,10,1,256]{3,2,1,0:T(2,128)(2,1)S(1)}, bf16[4,10,1,256]{3,2,1,0:T(2,128)(2,1)S(1)}, u32[]{:S(2)}, u32[]{:S(2)}) collective-permute-start(bf16[4,10,1,256]{3,2,1,0:T(2,128)(2,1)S(1)} %get-tuple-element.132), channel_id=1, source_target_pairs={{2,0},{4,2},{6,4},{8,6},{10,8},{12,10},{14,12},{0,14},{3,1},{5,3},... | collective-permute-start | bytes 61448 | tf_op jit(solution)/shard_map/ppermute | solution.py:29
  91.7 1.5 reshape.214
  97.8 1.4 reshape.215
  99.3 3.0 %convert_reduce_fusion.1 = (f32[4,32]{0,1:T(8,128)S(1)}, f32[4,32]{0,1:T(8,128)S(1)}, bf16[4,256,32,8]{1,0,3,2:T(4,128)(2,1)}) fusion(f32[4,256,32,8]{1,0,3,2:T(4,128)} %reshape.214, f32[4,256,32,8]{1,0,3,2:T(4,128)} %reshape.215, f32[32,8]{1,0:T(8,128)S(1)} %add.329), kind=kLoop, calls=%fused_computation.59 | loop fusion | flops 1834752 | bytes 2623488 | tf_op jit(solution)/shard_map/reduce_sum | solution.py:36
  102.4 2.5 all-reduce.9
  104.9 21.8 %all-reduce.3 = (f32[4,32]{1,0:T(4,128)S(1)}, f32[4,32]{1,0:T(4,128)S(1)}) all-reduce(f32[4,32]{1,0:T(4,128)S(1)} %get-tuple-element.39, f32[4,32]{1,0:T(4,128)S(1)} %get-tuple-element.40), channel_id=1, replica_groups=mesh['groups'=2,'blk'=8,'rows'=2] {'blk'}, use_global_device_ids=true, to_apply=%region_19.0 | all-reduce | flops 256 | bytes 2048 | tf_op jit(solution)/shard_map/psum | solution.py:13
  127.1 1.2 fusion.49
  128.4 1.3 collective-permute-start.8
  129.7 1.3 collective-permute-start.9
  131.0 1.8 collective-permute-done.9
  133.0 4.7 %collective-permute-start.11 = (bf16[4,10,1,256]{3,2,1,0:T(2,128)(2,1)S(1)}, bf16[4,10,1,256]{3,2,1,0:T(2,128)(2,1)S(1)}, u32[]{:S(2)}, u32[]{:S(2)}) collective-permute-start(bf16[4,10,1,256]{3,2,1,0:T(2,128)(2,1)S(1)} %get-tuple-element.128), channel_id=1, source_target_pairs={{2,0},{4,2},{6,4},{8,6},{10,8},{12,10},{14,12},{0,14},{3,1},{5,3},... | collective-permute-start | bytes 61448 | tf_op jit(solution)/shard_map/ppermute | solution.py:29
  137.7 1.9 collective-permute-done.10
  144.8 0.7 convert_reduce_fusion.4
  145.6 2.5 all-reduce.8
  148.1 21.8 %all-reduce.2 = (f32[4,32]{1,0:T(4,128)S(1)}, f32[4,32]{1,0:T(4,128)S(1)}) all-reduce(f32[4,32]{1,0:T(4,128)S(1)} %get-tuple-element.37, f32[4,32]{1,0:T(4,128)S(1)} %get-tuple-element.38), channel_id=1, replica_groups=mesh['groups'=2,'blk'=8,'rows'=2] {'blk'}, use_global_device_ids=true, to_apply=%region_25.0 | all-reduce | flops 256 | bytes 2048 | tf_op jit(solution)/shard_map/psum | solution.py:13
  170.7 1.3 collective-permute-start.12
  172.0 1.3 collective-permute-start.13
  173.3 1.8 collective-permute-done.13
  175.3 4.7 %collective-permute-start.15 = (bf16[4,10,1,256]{3,2,1,0:T(2,128)(2,1)S(1)}, bf16[4,10,1,256]{3,2,1,0:T(2,128)(2,1)S(1)}, u32[]{:S(2)}, u32[]{:S(2)}) collective-permute-start(bf16[4,10,1,256]{3,2,1,0:T(2,128)(2,1)S(1)} %get-tuple-element.124), channel_id=1, source_target_pairs={{2,0},{4,2},{6,4},{8,6},{10,8},{12,10},{14,12},{0,14},{3,1},{5,3},... | collective-permute-start | bytes 61448 | tf_op jit(solution)/shard_map/ppermute | solution.py:29
  180.1 1.9 collective-permute-done.14
  187.1 1.9 convert_reduce_fusion.3
  189.2 2.5 all-reduce.7
  191.6 21.8 %all-reduce.1 = (f32[4,32]{1,0:T(4,128)S(1)}, f32[4,32]{1,0:T(4,128)S(1)}) all-reduce(f32[4,32]{1,0:T(4,128)S(1)} %get-tuple-element.35, f32[4,32]{1,0:T(4,128)S(1)} %get-tuple-element.36), channel_id=1, replica_groups=mesh['groups'=2,'blk'=8,'rows'=2] {'blk'}, use_global_device_ids=true, to_apply=%region_31.0 | all-reduce | flops 256 | bytes 2048 | tf_op jit(solution)/shard_map/psum | solution.py:13
  213.9 1.2 fusion.60
  215.1 1.3 collective-permute-start.16
  216.4 1.3 collective-permute-start.17
  217.7 1.8 collective-permute-done.17
  219.7 4.7 %collective-permute-start.19 = (bf16[4,10,1,256]{3,2,1,0:T(2,128)(2,1)S(1)}, bf16[4,10,1,256]{3,2,1,0:T(2,128)(2,1)S(1)}, u32[]{:S(2)}, u32[]{:S(2)}) collective-permute-start(bf16[4,10,1,256]{3,2,1,0:T(2,128)(2,1)S(1)} %get-tuple-element.120), channel_id=1, source_target_pairs={{2,0},{4,2},{6,4},{8,6},{10,8},{12,10},{14,12},{0,14},{3,1},{5,3},... | collective-permute-start | bytes 61448 | tf_op jit(solution)/shard_map/ppermute | solution.py:29
  224.5 1.9 collective-permute-done.18
  230.1 0.6 fusion.35
  231.5 0.7 convert_reduce_fusion.2
  232.4 2.5 all-reduce.6
  234.8 21.8 %all-reduce = (f32[4,32]{1,0:T(4,128)S(1)}, f32[4,32]{1,0:T(4,128)S(1)}) all-reduce(f32[4,32]{1,0:T(4,128)S(1)} %get-tuple-element.33, f32[4,32]{1,0:T(4,128)S(1)} %get-tuple-element.34), channel_id=1, replica_groups=mesh['groups'=2,'blk'=8,'rows'=2] {'blk'}, use_global_device_ids=true, to_apply=%region_37.38 | all-reduce | flops 256 | bytes 2048 | tf_op jit(solution)/shard_map/psum | solution.py:13
  257.4 1.3 collective-permute-start.20
  258.7 1.3 collective-permute-start.21
  260.1 1.8 collective-permute-done.21
  262.0 4.7 %collective-permute-start.23 = (bf16[4,10,1,256]{3,2,1,0:T(2,128)(2,1)S(1)}, bf16[4,10,1,256]{3,2,1,0:T(2,128)(2,1)S(1)}, u32[]{:S(2)}, u32[]{:S(2)}) collective-permute-start(bf16[4,10,1,256]{3,2,1,0:T(2,128)(2,1)S(1)} %get-tuple-element.116), channel_id=1, source_target_pairs={{2,0},{4,2},{6,4},{8,6},{10,8},{12,10},{14,12},{0,14},{3,1},{5,3},... | collective-permute-start | bytes 61448 | tf_op jit(solution)/shard_map/ppermute | solution.py:29
  266.7 2.0 collective-permute-done.22
  273.5 1.0 fusion.61
  (189 shorter events, 30.6 us)
Async XLA Ops:
  0.0 84.5 %copy-start = (bf16[512,256]{1,0:T(8,128)(2,1)S(1)}, bf16[512,256]{1,0:T(8,128)(2,1)}, u32[]{:S(2)}) copy-start(bf16[512,256]{1,0:T(8,128)(2,1)} %param.16) | copy-start | bytes 786436
  0.0 28.0 %copy-start.2 = (bf16[4,8,32,512]{3,2,1,0:T(8,128)(2,1)S(1)}, bf16[4,8,32,512]{3,2,1,0:T(8,128)(2,1)}, u32[]{:S(2)}) copy-start(bf16[4,8,32,512]{3,2,1,0:T(8,128)(2,1)} %param.11) | copy-start | bytes 3145732
  0.0 28.0 %copy-start.28 = (f32[512]{0:T(512)S(1)}, f32[512]{0:T(512)}, u32[]{:S(2)}) copy-start(f32[512]{0:T(512)} %param.12) | copy-start | bytes 6148
  0.0 28.0 %copy-start.27 = (f32[512]{0:T(512)S(1)}, f32[512]{0:T(512)}, u32[]{:S(2)}) copy-start(f32[512]{0:T(512)} %param.13) | copy-start | bytes 6148
  28.0 6.6 %copy-start.3 = (bf16[5,3,3,256,256]{4,3,2,1,0:T(8,128)(2,1)S(1)}, bf16[5,3,3,256,256]{4,3,2,1,0:T(8,128)(2,1)}, u32[]{:S(2)}) copy-start(bf16[5,3,3,256,256]{4,3,2,1,0:T(8,128)(2,1)} %param.20) | copy-start | bytes 17694724
  28.8 8.4 %collective-permute-start = (bf16[4,1,32,512]{3,2,1,0:T(8,128)(2,1)S(1)}, bf16[4,1,32,512]{3,2,1,0:T(8,128)(2,1)S(1)}, u32[]{:S(2)}, u32[]{:S(2)}) collective-permute-start(bf16[4,1,32,512]{3,2,1,0:T(8,128)(2,1)S(1)} %get-tuple-element.81), channel_id=1, source_target_pairs={{0,1},{2,3},{4,5},{6,7},{8,9},{10,11},{12,13},{14,15},{16,17},{18,... | collective-permute-start | bytes 393224 | tf_op jit(solution)/shard_map/ppermute | solution.py:26
  30.4 6.9 %collective-permute-start.1 = (bf16[4,1,32,512]{3,2,1,0:T(8,128)(2,1)S(1)}, bf16[4,1,32,512]{3,2,1,0:T(8,128)(2,1)S(1)}, u32[]{:S(2)}, u32[]{:S(2)}) collective-permute-start(bf16[4,1,32,512]{3,2,1,0:T(8,128)(2,1)S(1)} %get-tuple-element.82), channel_id=1, source_target_pairs={{1,0},{3,2},{5,4},{7,6},{9,8},{11,10},{13,12},{15,14},{17,16},{19,... | collective-permute-start | bytes 393224 | tf_op jit(solution)/shard_map/ppermute | solution.py:29
  34.7 2.6 copy-start.25
  34.7 8.1 %copy-start.26 = (f32[5,256]{1,0:T(8,128)S(1)}, f32[5,256]{1,0:T(8,128)}, u32[]{:S(2)}) copy-start(f32[5,256]{1,0:T(8,128)} %param.18) | copy-start | bytes 15364
  34.7 8.1 %copy-start.23 = (f32[256]{0:T(256)S(1)}, f32[256]{0:T(256)}, u32[]{:S(2)}) copy-start(f32[256]{0:T(256)} %param.15) | copy-start | bytes 3076
  38.0 8.2 %collective-permute-start.2 = (bf16[4,10,1,512]{3,2,1,0:T(2,128)(2,1)}, bf16[4,10,1,512]{3,2,1,0:T(2,128)(2,1)}, u32[]{:S(2)}, u32[]{:S(2)}) collective-permute-start(bf16[4,10,1,512]{3,2,1,0:T(2,128)(2,1)} %get-tuple-element.76), channel_id=1, source_target_pairs={{0,2},{2,4},{4,6},{6,8},{8,10},{10,12},{12,14},{14,0},{1,3},{3,5},... | collective-permute-start | bytes 122888 | tf_op jit(solution)/shard_map/ppermute | solution.py:26
  38.0 8.2 %collective-permute-start.3 = (bf16[4,10,1,512]{3,2,1,0:T(2,128)(2,1)S(1)}, bf16[4,10,1,512]{3,2,1,0:T(2,128)(2,1)}, u32[]{:S(2)}, u32[]{:S(2)}) collective-permute-start(bf16[4,10,1,512]{3,2,1,0:T(2,128)(2,1)S(1)} %get-tuple-element.77), channel_id=1, source_target_pairs={{2,0},{4,2},{6,4},{8,6},{10,8},{12,10},{14,12},{0,14},{3,1},{5,3},... | collective-permute-start | bytes 122888 | tf_op jit(solution)/shard_map/ppermute | solution.py:29
  48.9 1.1 copy-start.22
  50.0 1.1 copy-start.21
  56.2 28.4 %copy-start.29 = (f32[256]{0:T(256)S(1)}, f32[256]{0:T(256)}, u32[]{:S(2)}) copy-start(f32[256]{0:T(256)} %param.17) | copy-start | bytes 3076
  81.9 9.3 %copy-start.24 = (f32[5,256]{1,0:T(8,128)S(1)}, f32[5,256]{1,0:T(8,128)}, u32[]{:S(2)}) copy-start(f32[5,256]{1,0:T(8,128)} %param.21) | copy-start | bytes 15364
  81.9 3.1 %collective-permute-start.4 = (bf16[4,1,32,256]{3,2,1,0:T(8,128)(2,1)S(1)}, bf16[4,1,32,256]{3,2,1,0:T(8,128)(2,1)S(1)}, u32[]{:S(2)}, u32[]{:S(2)}) collective-permute-start(bf16[4,1,32,256]{3,2,1,0:T(8,128)(2,1)S(1)} %get-tuple-element.156), channel_id=1, source_target_pairs={{0,1},{2,3},{4,5},{6,7},{8,9},{10,11},{12,13},{14,15},{16,17},{18,... | collective-permute-start | bytes 196616 | tf_op jit(solution)/shard_map/ppermute | solution.py:26
  83.2 3.1 %collective-permute-start.5 = (bf16[4,1,32,256]{3,2,1,0:T(8,128)(2,1)S(1)}, bf16[4,1,32,256]{3,2,1,0:T(8,128)(2,1)S(1)}, u32[]{:S(2)}, u32[]{:S(2)}) collective-permute-start(bf16[4,1,32,256]{3,2,1,0:T(8,128)(2,1)S(1)} %get-tuple-element.157), channel_id=1, source_target_pairs={{1,0},{3,2},{5,4},{7,6},{9,8},{11,10},{13,12},{15,14},{17,16},{19,... | collective-permute-start | bytes 196616 | tf_op jit(solution)/shard_map/ppermute | solution.py:29
  86.5 6.8 %collective-permute-start.6 = (bf16[4,10,1,256]{3,2,1,0:T(2,128)(2,1)S(1)}, bf16[4,10,1,256]{3,2,1,0:T(2,128)(2,1)S(1)}, u32[]{:S(2)}, u32[]{:S(2)}) collective-permute-start(bf16[4,10,1,256]{3,2,1,0:T(2,128)(2,1)S(1)} %get-tuple-element.131), channel_id=1, source_target_pairs={{0,2},{2,4},{4,6},{6,8},{8,10},{10,12},{12,14},{14,0},{1,3},{3,5},... | collective-permute-start | bytes 61448 | tf_op jit(solution)/shard_map/ppermute | solution.py:26
  86.5 6.7 %collective-permute-start.7 = (bf16[4,10,1,256]{3,2,1,0:T(2,128)(2,1)S(1)}, bf16[4,10,1,256]{3,2,1,0:T(2,128)(2,1)S(1)}, u32[]{:S(2)}, u32[]{:S(2)}) collective-permute-start(bf16[4,10,1,256]{3,2,1,0:T(2,128)(2,1)S(1)} %get-tuple-element.132), channel_id=1, source_target_pairs={{2,0},{4,2},{6,4},{8,6},{10,8},{12,10},{14,12},{0,14},{3,1},{5,3},... | collective-permute-start | bytes 61448 | tf_op jit(solution)/shard_map/ppermute | solution.py:29
  94.3 1.0 copy-start.20
  94.8 1.1 copy-start.19
  95.9 1.0 copy-start.10
  128.4 2.6 collective-permute-start.8
  129.7 3.1 %collective-permute-start.9 = (bf16[4,1,32,256]{3,2,1,0:T(8,128)(2,1)S(1)}, bf16[4,1,32,256]{3,2,1,0:T(8,128)(2,1)S(1)}, u32[]{:S(2)}, u32[]{:S(2)}) collective-permute-start(bf16[4,1,32,256]{3,2,1,0:T(8,128)(2,1)S(1)} %get-tuple-element.152), channel_id=1, source_target_pairs={{1,0},{3,2},{5,4},{7,6},{9,8},{11,10},{13,12},{15,14},{17,16},{19,... | collective-permute-start | bytes 196616 | tf_op jit(solution)/shard_map/ppermute | solution.py:29
  132.9 6.8 %collective-permute-start.10 = (bf16[4,10,1,256]{3,2,1,0:T(2,128)(2,1)S(1)}, bf16[4,10,1,256]{3,2,1,0:T(2,128)(2,1)S(1)}, u32[]{:S(2)}, u32[]{:S(2)}) collective-permute-start(bf16[4,10,1,256]{3,2,1,0:T(2,128)(2,1)S(1)} %get-tuple-element.127), channel_id=1, source_target_pairs={{0,2},{2,4},{4,6},{6,8},{8,10},{10,12},{12,14},{14,0},{1,3},{3,5},... | collective-permute-start | bytes 61448 | tf_op jit(solution)/shard_map/ppermute | solution.py:26
  133.0 6.7 %collective-permute-start.11 = (bf16[4,10,1,256]{3,2,1,0:T(2,128)(2,1)S(1)}, bf16[4,10,1,256]{3,2,1,0:T(2,128)(2,1)S(1)}, u32[]{:S(2)}, u32[]{:S(2)}) collective-permute-start(bf16[4,10,1,256]{3,2,1,0:T(2,128)(2,1)S(1)} %get-tuple-element.128), channel_id=1, source_target_pairs={{2,0},{4,2},{6,4},{8,6},{10,8},{12,10},{14,12},{0,14},{3,1},{5,3},... | collective-permute-start | bytes 61448 | tf_op jit(solution)/shard_map/ppermute | solution.py:29
  140.7 1.0 copy-start.18
  141.2 1.1 copy-start.17
  142.3 1.0 copy-start.9
  170.7 2.6 collective-permute-start.12
  172.0 3.1 %collective-permute-start.13 = (bf16[4,1,32,256]{3,2,1,0:T(8,128)(2,1)S(1)}, bf16[4,1,32,256]{3,2,1,0:T(8,128)(2,1)S(1)}, u32[]{:S(2)}, u32[]{:S(2)}) collective-permute-start(bf16[4,1,32,256]{3,2,1,0:T(8,128)(2,1)S(1)} %get-tuple-element.147), channel_id=1, source_target_pairs={{1,0},{3,2},{5,4},{7,6},{9,8},{11,10},{13,12},{15,14},{17,16},{19,... | collective-permute-start | bytes 196616 | tf_op jit(solution)/shard_map/ppermute | solution.py:29
  175.2 6.8 %collective-permute-start.14 = (bf16[4,10,1,256]{3,2,1,0:T(2,128)(2,1)S(1)}, bf16[4,10,1,256]{3,2,1,0:T(2,128)(2,1)S(1)}, u32[]{:S(2)}, u32[]{:S(2)}) collective-permute-start(bf16[4,10,1,256]{3,2,1,0:T(2,128)(2,1)S(1)} %get-tuple-element.123), channel_id=1, source_target_pairs={{0,2},{2,4},{4,6},{6,8},{8,10},{10,12},{12,14},{14,0},{1,3},{3,5},... | collective-permute-start | bytes 61448 | tf_op jit(solution)/shard_map/ppermute | solution.py:26
  175.3 6.7 %collective-permute-start.15 = (bf16[4,10,1,256]{3,2,1,0:T(2,128)(2,1)S(1)}, bf16[4,10,1,256]{3,2,1,0:T(2,128)(2,1)S(1)}, u32[]{:S(2)}, u32[]{:S(2)}) collective-permute-start(bf16[4,10,1,256]{3,2,1,0:T(2,128)(2,1)S(1)} %get-tuple-element.124), channel_id=1, source_target_pairs={{2,0},{4,2},{6,4},{8,6},{10,8},{12,10},{14,12},{0,14},{3,1},{5,3},... | collective-permute-start | bytes 61448 | tf_op jit(solution)/shard_map/ppermute | solution.py:29
  183.1 1.0 copy-start.16
  183.6 1.1 copy-start.15
  184.7 1.0 copy-start.8
  187.1 26.7 %copy-start.4 = (bf16[4,8,32,256]{3,2,1,0:T(8,128)(2,1)S(1)}, bf16[4,8,32,256]{3,2,1,0:T(8,128)(2,1)}, u32[]{:S(2)}) copy-start(bf16[4,8,32,256]{3,2,1,0:T(8,128)(2,1)} %get-tuple-element.48) | copy-start | bytes 1572868
  215.1 2.6 collective-permute-start.16
  216.4 3.1 %collective-permute-start.17 = (bf16[4,1,32,256]{3,2,1,0:T(8,128)(2,1)S(1)}, bf16[4,1,32,256]{3,2,1,0:T(8,128)(2,1)S(1)}, u32[]{:S(2)}, u32[]{:S(2)}) collective-permute-start(bf16[4,1,32,256]{3,2,1,0:T(8,128)(2,1)S(1)} %get-tuple-element.142), channel_id=1, source_target_pairs={{1,0},{3,2},{5,4},{7,6},{9,8},{11,10},{13,12},{15,14},{17,16},{19,... | collective-permute-start | bytes 196616 | tf_op jit(solution)/shard_map/ppermute | solution.py:29
  219.6 6.8 %collective-permute-start.18 = (bf16[4,10,1,256]{3,2,1,0:T(2,128)(2,1)S(1)}, bf16[4,10,1,256]{3,2,1,0:T(2,128)(2,1)S(1)}, u32[]{:S(2)}, u32[]{:S(2)}) collective-permute-start(bf16[4,10,1,256]{3,2,1,0:T(2,128)(2,1)S(1)} %get-tuple-element.119), channel_id=1, source_target_pairs={{0,2},{2,4},{4,6},{6,8},{8,10},{10,12},{12,14},{14,0},{1,3},{3,5},... | collective-permute-start | bytes 61448 | tf_op jit(solution)/shard_map/ppermute | solution.py:26
  219.7 6.7 %collective-permute-start.19 = (bf16[4,10,1,256]{3,2,1,0:T(2,128)(2,1)S(1)}, bf16[4,10,1,256]{3,2,1,0:T(2,128)(2,1)S(1)}, u32[]{:S(2)}, u32[]{:S(2)}) collective-permute-start(bf16[4,10,1,256]{3,2,1,0:T(2,128)(2,1)S(1)} %get-tuple-element.120), channel_id=1, source_target_pairs={{2,0},{4,2},{6,4},{8,6},{10,8},{12,10},{14,12},{0,14},{3,1},{5,3},... | collective-permute-start | bytes 61448 | tf_op jit(solution)/shard_map/ppermute | solution.py:29
  227.5 1.0 copy-start.14
  228.0 1.1 copy-start.13
  229.1 1.0 copy-start.7
  257.4 2.6 collective-permute-start.20
  258.7 3.1 %collective-permute-start.21 = (bf16[4,1,32,256]{3,2,1,0:T(8,128)(2,1)S(1)}, bf16[4,1,32,256]{3,2,1,0:T(8,128)(2,1)S(1)}, u32[]{:S(2)}, u32[]{:S(2)}) collective-permute-start(bf16[4,1,32,256]{3,2,1,0:T(8,128)(2,1)S(1)} %get-tuple-element.137), channel_id=1, source_target_pairs={{1,0},{3,2},{5,4},{7,6},{9,8},{11,10},{13,12},{15,14},{17,16},{19,... | collective-permute-start | bytes 196616 | tf_op jit(solution)/shard_map/ppermute | solution.py:29
  262.0 6.8 %collective-permute-start.22 = (bf16[4,10,1,256]{3,2,1,0:T(2,128)(2,1)S(1)}, bf16[4,10,1,256]{3,2,1,0:T(2,128)(2,1)S(1)}, u32[]{:S(2)}, u32[]{:S(2)}) collective-permute-start(bf16[4,10,1,256]{3,2,1,0:T(2,128)(2,1)S(1)} %get-tuple-element.115), channel_id=1, source_target_pairs={{0,2},{2,4},{4,6},{6,8},{8,10},{10,12},{12,14},{14,0},{1,3},{3,5},... | collective-permute-start | bytes 61448 | tf_op jit(solution)/shard_map/ppermute | solution.py:26
  262.0 6.7 %collective-permute-start.23 = (bf16[4,10,1,256]{3,2,1,0:T(2,128)(2,1)S(1)}, bf16[4,10,1,256]{3,2,1,0:T(2,128)(2,1)S(1)}, u32[]{:S(2)}, u32[]{:S(2)}) collective-permute-start(bf16[4,10,1,256]{3,2,1,0:T(2,128)(2,1)S(1)} %get-tuple-element.116), channel_id=1, source_target_pairs={{2,0},{4,2},{6,4},{8,6},{10,8},{12,10},{14,12},{0,14},{3,1},{5,3},... | collective-permute-start | bytes 61448 | tf_op jit(solution)/shard_map/ppermute | solution.py:29
  269.8 1.0 copy-start.12
  270.3 1.1 copy-start.11
  271.4 1.0 copy-start.6
  272.4 1.0 copy-start.5
  272.4 2.0 copy-start.1
